TPU v7x, 128 devices: a whole 4x4x4 slice. The times are simulated.
128 devices in a mesh: lon: 8 (over z, core), lat: 4 (over y), mem: 4 (over x).
Axes of the slice: x: 4, y: 4, z: 4, core: 2. Of those that a mesh axis runs over, the one named last changes fastest.
Arguments:
- ensemble: bfloat16 [80, 4, 4, 512, 512], P('mem', None, None, 'lon', 'lat'), may hold values from -6 to 6
- huber: float32 [4, 4, 512, 512], P(None, None, 'lon', 'lat'), may hold values from 0.1 to 1
- innovation: float32 [4, 4, 512, 512], P(None, None, 'lon', 'lat'), may hold values from -6 to 6
- sea_mask: int32 [128, 128], P('lon', 'lat'), may hold values 0 or 1
Outputs:
- control: float32 [80, 4, 128, 128], P('mem', None, 'lon', 'lat')
- gradient: float32 [80, 4, 128, 128], P('mem', None, 'lon', 'lat')
All inputs are finite; a program needn't handle non-finite values. No bound on the sum of `sea_mask` on one device may be relied on, other than what follows from the above.
Results may differ from a plain program's by a relative error of at most 0.013.
Values may be sent and summed in bfloat16 or wider, within the bound.
A program may use at most 128 MiB of HBM per device.

v0:
```python
import math

import jax
import jax.numpy as jnp
import numpy as np
from jax import lax
from jax.experimental import pallas as pl
from jax.experimental.pallas import tpu as pltpu
from jax.sharding import PartitionSpec as P


MEMBERS, VARS, LEV = 80, 4, 4
ITERS = 3
GROUPS, PER = 5, 4
OWN_X, OWN_Y = 16, 32
FINE_X, FINE_Y = 64, 128
CHUNK = 16
SX_WEIGHT = (1.0, 2.0, 3.0, 2.0, 1.0)
SY_WEIGHT = (1.0, 2.0, 2.0, 2.0, 1.0)
S_SCALE = 1e-4
MESH = pl.DeviceIdType.MESH
BF, F32 = jnp.bfloat16, jnp.float32


def powers(count, variant):
    where = np.arange(-9, count + 9)
    inside = np.ones(where.shape)
    if variant == 0:
        inside = (where >= 0).astype(float)
    if variant == 2:
        inside = (where < count).astype(float)
    size = where.size
    table = np.eye(size) + 2 * (np.eye(size, k=1) + np.eye(size, k=-1))
    table = inside[:, None] * table * inside[None, :]
    result = [np.diag(inside)]
    for _ in range(4):
        result.append(result[-1] @ table)
    return result


def hat(fine):
    position = (np.arange(fine) + 0.5) / 4 - 0.5
    return lambda c: np.maximum(0.0, 1 - np.abs(c - position))


def window_rows():
    own = [(m, r) for m in range(PER) for r in range(16)]
    halo = [(m, r) for m in range(PER) for r in [*range(-5, 0), *range(16, 21)]]
    return own + halo + [(-1, 0)] * 8


def a_rows():
    return [(m, r) for m in range(PER) for r in range(-1, 17)] + [(-1, 0)] * 8


def b_rows():
    top = [(m, r, 0) for m in range(PER) for r in range(-1, 9)]
    bottom = [(m, r, 0) for m in range(PER) for r in range(7, 17)]
    return top + bottom


def full_rows():
    own = b_rows()
    own = own[:40] + [(m if r > 8 else -1, r, 0) for m, r, _ in own[40:]]
    before = [(m, r - 16, -1) for m in range(PER) for r in range(7, 17)]
    after = [(m, r + 16, 1) for m in range(PER) for r in range(-1, 9)]
    return own + before + after


def window_lanes():
    own = [(l, c) for l in range(LEV) for c in range(32)]
    halo = [(l, c) for l in range(LEV) for c in [*range(-5, 0), *range(32, 37)]]
    return own + halo + [(-1, 0)] * 88


def a_lanes():
    return [(l, c) for l in range(LEV) for c in range(-1, 33)] + [(-1, 0)] * 120


def strip(cells, source):
    return [(l, c, source) for l in range(LEV) for c in cells]


def b_lanes():
    gap = [(-1, 0, 0)]
    first = strip(range(-1, 9), 0) + strip(range(9, 23), 0) + gap * 32
    right, left = strip(range(23, 33), 0), strip(range(-1, 9), 0)
    return first + right + gap * 4 + right + gap * 4 + left


def full_lanes():
    gap = [(-1, 0, 0)]
    first = strip(range(-1, 9), 0) + strip(range(9, 23), 0) + gap * 32
    before, after = strip(range(-9, 1), -1), strip(range(31, 41), 1)
    return first + before + gap * 4 + strip(range(23, 33), 0) + gap * 4 + after


def exists(source, variant):
    return not ((source == -1 and variant == 0) or (source == 1 and variant == 2))


def tables():
    wr, ar, fr = window_rows(), a_rows(), full_rows()
    wl, al, fl = window_lanes(), a_lanes(), full_lanes()
    sxf = np.zeros((3, 5, 80, 128))
    sxb = np.zeros((3, 5, 112, 256))
    for variant in range(3):
        powered = powers(OWN_X, variant)
        for k in range(5):
            for i, (m, r) in enumerate(ar):
                for j, (n, q) in enumerate(wr):
                    if m == n and m >= 0:
                        sxf[variant, k, i, j] = SX_WEIGHT[k] * powered[k][r + 9, q + 9]
            for i, (m, r) in enumerate(wr):
                for j, (n, q, source) in enumerate(fr):
                    if m == n and m >= 0 and exists(source, variant):
                        sxb[variant, k, i, j] = SX_WEIGHT[k] * powered[k][r + 9, q + 9]
    base = np.zeros((3, 5, 64, 128))
    for variant in range(3):
        powered = powers(OWN_Y, variant)
        for k in range(5):
            base[variant, k, 7:57, 7:57] = SY_WEIGHT[k] * powered[4 - k]
    alive = np.zeros((3, 256, 128))
    for variant in range(3):
        for i, (l, c, source) in enumerate(fl):
            alive[variant, i, :] = float(l >= 0 and exists(source, variant))
    pick_w, pick_a, pick_f = (np.zeros((256, 128)) for _ in range(3))
    for table, order in ((pick_w, wl), (pick_a, al), (pick_f, fl)):
        for i, item in enumerate(order):
            if item[0] >= 0:
                table[i, item[1] + 16] = 1
    level = lambda order: np.array([item[0] for item in order])
    same = lambda one, two: ((level(one)[:, None] == level(two)[None, :]) & (level(one)[:, None] >= 0)).astype(float)
    same_wa, same_fw = same(wl, al), same(fl, wl)
    weight_x, weight_y = hat(FINE_X), hat(FINE_Y)
    pxf, pxt = np.zeros((256, 128)), np.zeros((80, 256))
    for j, (m, r) in enumerate(ar):
        if m >= 0:
            pxf[m * 64 : m * 64 + 64, j] = weight_x(r)
    for j, (m, r, _) in enumerate(b_rows()):
        pxt[j, m * 64 : m * 64 + 64] = weight_x(r)
    pyf, pyt = np.zeros((256, 512)), np.zeros((512, 256))
    for j, (l, c) in enumerate(al):
        if l >= 0:
            pyf[j, l * 128 : l * 128 + 128] = weight_y(c)
    for j, (l, c, _) in enumerate(b_lanes()):
        if l >= 0:
            pyt[l * 128 : l * 128 + 128, j] = weight_y(c)
    mask_x, mask_y = np.zeros((80, 16)), np.zeros((32, 256))
    for i, (m, r, _) in enumerate(b_rows()):
        if 0 <= r < 16:
            mask_x[i, r] = 1
    for j, (l, c, _) in enumerate(b_lanes()):
        if l >= 0 and 0 <= c < 32:
            mask_y[c, j] = 1
    home = lambda value, count: -1 if value < 0 else (1 if value >= count else 0)
    take_x, take_y = np.zeros((112, 256)), np.zeros((256, 256))
    for i, (m, r) in enumerate(wr):
        for j, (n, q, source) in enumerate(fr):
            if m == n and m >= 0 and r == q and source == home(r, 16):
                take_x[i, j] = 1
    for j, (l, c) in enumerate(wl):
        for i, (n, q, source) in enumerate(fl):
            if l == n and l >= 0 and c == q and source == home(c, 32):
                take_y[i, j] = 1
    named = dict(
        sxf=sxf, sxb=sxb, base=base, alive=alive, pick_w=pick_w, pick_a=pick_a, pick_f=pick_f, same_wa=same_wa,
        same_fw=same_fw, pxf=pxf, pxt=pxt, pyf=pyf, pyt=pyt, mask_x=mask_x, mask_y=mask_y, take_x=take_x, take_y=take_y,
    )
    return {name: np.asarray(value, np.float32).astype(BF) for name, value in named.items()}


TABLES = tables()
NAMES = tuple(TABLES)
BY_LON, BY_LAT = ("sxf", "sxb"), ("base", "alive")


def dot(a, b):
    return lax.dot_general(a, b, (((1,), (0,)), ((), ())), preferred_element_type=F32)


def dot_nt(a, b):
    return lax.dot_general(a, b, (((1,), (1,)), ((), ())), preferred_element_type=F32)


def kernel(sizes, *refs):
    n_lon, n_lat, n_mem = sizes
    names = ["ens_hbm", "hub_hbm", "inn_hbm", "mask_ref", *(n + "_hbm" for n in NAMES), "out_c", "out_g", "ens", "hub", "inn"]
    names += [*NAMES, "syf", "syb", "win_mask", "grad", "ag", "ctl", "wbuf", "spread", "mis", "rs_own", "rs_send", "rs_recv"]
    names += ["h_send", "h_recv", "sc_send", "sc_m", "sc_y", "sc_x"]
    names += ["in_sem", "ens_sem", "hs_sem", "hr_sem", "rss_sem", "rsr_sem", "ags_sem", "agr_sem", "scs_sem", "scr_sem"]
    r = dict(zip(names, refs, strict=True))
    lon, lat, mem = lax.axis_index("lon"), lax.axis_index("lat"), lax.axis_index("mem")
    scale = 1.0 / math.sqrt(MEMBERS - 1)

    def at(d_lon=0, d_lat=0, d_mem=0):
        return {
            "lon": lax.rem(lon + (d_lon + n_lon), n_lon),
            "lat": lax.rem(lat + (d_lat + n_lat), n_lat),
            "mem": lax.rem(mem + (d_mem + n_mem), n_mem),
        }

    variant_x = jnp.where(lon == 0, 0, jnp.where(lon == n_lon - 1, 2, 1))
    variant_y = jnp.where(lat == 0, 0, jnp.where(lat == n_lat - 1, 2, 1))
    loads = {}
    order = ["base", "alive", "pick_w", "pick_a", "pick_f", "same_wa", "same_fw", "hub", "inn"]
    for i, name in enumerate([*order, *(n for n in NAMES if n not in order)]):
        source = r[name + "_hbm"]
        if name in BY_LON:
            source = source.at[variant_x]
        if name in BY_LAT:
            source = source.at[variant_y]
        loads[name] = pltpu.make_async_copy(source, r[name], r["in_sem"].at[i])
        loads[name].start()
    for g in range(GROUPS):
        part = pl.ds(g * PER, PER)
        pltpu.make_async_copy(r["ens_hbm"].at[part], r["ens"].at[part], r["ens_sem"].at[g]).start()

    barrier = pltpu.get_barrier_semaphore()
    partners = [at(d_mem=d) for d in range(1, n_mem)]
    partners += [at(d_lat=d) for d in range(1, n_lat)]
    partners += [at(d_lon=d) for d in range(1, n_lon)]
    partners += [at(d_lon=dx, d_lat=dy) for dx in (-1, 1) for dy in (-1, 1)]
    for partner in partners:
        pl.semaphore_signal(barrier, inc=1, device_id=partner, device_id_type=MESH)

    lane = lax.broadcasted_iota(jnp.int32, (40, 128), 1)

    for name in order[:7]:
        loads[name].wait()

    @pl.loop(0, 5)
    def _(k):
        base = r["base"][k]
        base = jnp.concatenate([base, jnp.zeros_like(base)], axis=0)
        to_a = dot_nt(base, r["pick_a"][...]).astype(BF)
        to_w = dot_nt(base, r["pick_w"][...]).astype(BF)
        r["syf"][k] = (dot(r["pick_w"][...], to_a).astype(BF) * r["same_wa"][...]).astype(BF)
        spread_f = dot(r["pick_f"][...] * r["alive"][...], to_w).astype(BF)
        r["syb"][k] = (spread_f * r["same_fw"][...]).astype(BF)

    for name in ("hub", "inn"):
        loads[name].wait()

    @pl.loop(0, LEV)
    def _(l):
        for v in range(VARS):
            r["mis"][0, l, v] = (r["hub"][v, l] * r["inn"][v, l]).astype(BF)

    for name in NAMES:
        if name not in order:
            loads[name].wait()
    pl.semaphore_wait(barrier, len(partners))

    def send_strips(e, g, b):
        first, second = b[:, :128], b[:, 128:]
        top, bottom = second[:40], second[40:]
        turned = pltpu.roll(bottom, 64, 1)
        out = r["h_send"].at[e, g]
        out[0] = first[:40].astype(BF)
        out[1] = top.astype(BF)
        out[2] = first[40:].astype(BF)
        out[3] = bottom.astype(BF)
        out[4] = jnp.where(lane < 64, turned, top).astype(BF)
        out[5] = jnp.where(lane < 64, top, turned).astype(BF)
        plan = (
            (4, 1, 5, (0, -1)),
            (5, 1, 4, (0, 1)),
            (4, 1, 9, (-1, -1)),
            (4, 1, 7, (1, -1)),
            (5, 1, 8, (-1, 1)),
            (5, 1, 6, (1, 1)),
            (0, 2, 2, (-1, 0)),
            (2, 2, 0, (1, 0)),
        )
        for source, count, target, (dx, dy) in plan:
            pltpu.make_async_remote_copy(
                src_ref=r["h_send"].at[e, g, pl.ds(source, count)],
                dst_ref=r["h_recv"].at[e, g, pl.ds(target, count)],
                send_sem=r["hs_sem"].at[e],
                recv_sem=r["hr_sem"].at[e, g],
                device_id=at(d_lon=dx, d_lat=dy),
                device_id_type=MESH,
            ).start()

    def adjoint_group(e, g):
        for c in range(FINE_X // CHUNK):
            rows = pl.ds(c * CHUNK, CHUNK)
            for l in range(LEV):
                weights = [r["mis"][e, l, v, rows].astype(F32) for v in range(VARS)]
                for m in range(PER):
                    total = sum(
                        r["ens"][g * PER + m, v, l, rows].astype(F32) * weights[v] for v in range(VARS)
                    )
                    r["spread"][pl.ds(m * 64 + c * CHUNK, CHUNK), l * 128 : l * 128 + 128] = total.astype(BF)
        coarse = dot(r["pxt"][...], r["spread"][...]).astype(BF)
        send_strips(e, g, dot(coarse, r["pyt"][...]) * scale)

    def assembled(e, g):
        pltpu.make_async_copy(r["h_recv"].at[e, g], r["h_recv"].at[e, g], r["hr_sem"].at[e, g]).wait()
        own = [r["h_send"][e, g, i].astype(F32) for i in range(4)]
        got = [r["h_recv"][e, g, i].astype(F32) for i in range(10)]

        def second(before, middle, after, turn):
            if turn:
                before, after = pltpu.roll(before, 64, 1), pltpu.roll(after, 64, 1)
            return jnp.where(lane < 42, before, jnp.where(lane < 86, middle, after))

        first = jnp.concatenate([own[0], own[2], got[0], got[2]], axis=0)
        other = jnp.concatenate(
            [
                second(got[4], own[1], got[5], False),
                second(got[4], own[3], got[5], True),
                second(got[6], got[1], got[7], True),
                second(got[8], got[3], got[9], False),
            ],
            axis=0,
        )
        return jnp.concatenate([first, other], axis=1).astype(BF)

    def smoothed(e, g):
        field = assembled(e, g)
        total = None
        for k in range(5):
            part = dot(r["sxb"][k, :, :160], field).astype(BF)
            part = dot(part, r["syb"][k])
            total = part if total is None else total + part
        return total * r["win_mask"][...]

    mask = r["mask_ref"][...].astype(F32).astype(BF)
    mask_rows = dot(r["mask_x"][...], mask).astype(BF)
    send_strips(0, GROUPS, dot(mask_rows, r["mask_y"][...]))

    @pl.loop(0, GROUPS)
    def _(g):
        part = pl.ds(g * PER, PER)
        pltpu.make_async_copy(r["ens_hbm"].at[part], r["ens"].at[part], r["ens_sem"].at[g]).wait()
        adjoint_group(0, g)

    picked = dot(r["take_x"][:, :160], assembled(0, GROUPS)).astype(BF)
    r["win_mask"][...] = dot(picked, r["take_y"][...]) * S_SCALE

    @pl.loop(0, GROUPS)
    def _(g):
        r["grad"][g] = -smoothed(0, g)
        r["ctl"][g] = jnp.zeros((64, 128), F32)

    row8 = lax.broadcasted_iota(jnp.int32, (8, 128), 0)

    def scalar_send(it, stage, buffer, targets):
        for slot, target in enumerate(targets):
            pltpu.make_async_remote_copy(
                src_ref=r["sc_send"].at[it, stage],
                dst_ref=buffer.at[it, slot],
                send_sem=r["scs_sem"].at[it, stage],
                recv_sem=r["scr_sem"].at[it, stage],
                device_id=target,
                device_id_type=MESH,
            ).start()

    def scalar_sum(it, stage, buffer, count):
        pltpu.make_async_copy(buffer.at[it], buffer.at[it], r["scr_sem"].at[it, stage]).wait()
        total = r["sc_send"][it, stage]
        for slot in range(count):
            total = total + buffer[it, slot]
        return total

    @pl.loop(0, ITERS)
    def _(it):
        squares = jnp.zeros((8, 128), F32)

        def fine_weights(g, squares):
            own = r["grad"][g, :64, :128]
            squares = squares + jnp.sum((own * own).reshape(8, 8, 128), axis=0)
            field = r["grad"][g].astype(BF)
            total = None
            for k in range(5):
                part = dot(r["sxf"][k, :, :112], field).astype(BF)
                part = dot(part, r["syf"][k])
                total = part if total is None else total + part
            coarse = (total * S_SCALE).astype(BF)
            fine = dot(coarse, r["pyf"][...]).astype(BF)
            fine = dot(r["pxf"][:, :80], fine).astype(BF)
            for l in range(LEV):
                r["wbuf"][l, g] = fine[:, l * 128 : l * 128 + 128]
            return squares

        squares = lax.fori_loop(0, GROUPS, fine_weights, squares)

        for step, away in enumerate((2, 1, 3, 0)):
            level = lax.rem(mem + away, n_mem)

            @pl.loop(0, FINE_X // CHUNK)
            def _(c):
                start = pl.multiple_of(c * CHUNK, CHUNK)
                rows = pl.ds(start, CHUNK)
                sums = [jnp.zeros((CHUNK, 128), F32) for _ in range(VARS)]
                for m in range(GROUPS * PER):
                    place = pl.ds(pl.multiple_of((m % PER) * 64 + start, CHUNK), CHUNK)
                    weight = r["wbuf"][level, m // PER, place].astype(F32)
                    for v in range(VARS):
                        sums[v] = sums[v] + r["ens"][m, v, level, rows].astype(F32) * weight
                for v in range(VARS):
                    if away:
                        r["rs_send"][it, step, v, rows] = sums[v].astype(BF)
                    else:
                        r["rs_own"][v, rows] = sums[v]

            if away:
                pltpu.make_async_remote_copy(
                    src_ref=r["rs_send"].at[it, step],
                    dst_ref=r["rs_recv"].at[it, step],
                    send_sem=r["rss_sem"].at[it],
                    recv_sem=r["rsr_sem"].at[it],
                    device_id=at(d_mem=away),
                    device_id_type=MESH,
                ).start()
        pltpu.make_async_copy(r["rs_recv"].at[it], r["rs_recv"].at[it], r["rsr_sem"].at[it]).wait()

        def misfit_rows(c, energy):
            rows = pl.ds(pl.multiple_of(c * CHUNK, CHUNK), CHUNK)
            for v in range(VARS):
                total = r["rs_own"][v, rows]
                for step in range(3):
                    total = total + r["rs_recv"][it, step, v, rows].astype(F32)
                total = total * scale
                rounded = (r["hub"][v, mem, rows] * total).astype(BF)
                r["mis"][it + 1, mem, v, rows] = rounded
                product = rounded.astype(F32) * total
                energy = energy + product[:8] + product[8:]
            return energy

        energy = lax.fori_loop(0, FINE_X // CHUNK, misfit_rows, jnp.zeros((8, 128), F32))
        for away in (2, 1, 3):
            pltpu.make_async_remote_copy(
                src_ref=r["mis"].at[it + 1, mem],
                dst_ref=r["mis"].at[it + 1, mem],
                send_sem=r["ags_sem"].at[it],
                recv_sem=r["agr_sem"].at[it],
                device_id=at(d_mem=away),
                device_id_type=MESH,
            ).start()
        squares = jnp.sum(squares, axis=0, keepdims=True)
        energy = jnp.sum(energy, axis=0, keepdims=True)
        r["sc_send"][it, 0] = jnp.where(row8 == 0, squares, jnp.where(row8 == 1, energy, 0.0))
        scalar_send(it, 0, r["sc_m"], [at(d_mem=d) for d in range(1, n_mem)])
        pltpu.make_async_copy(r["rs_recv"].at[it], r["rs_recv"].at[it], r["agr_sem"].at[it]).wait()
        r["sc_send"][it, 1] = scalar_sum(it, 0, r["sc_m"], n_mem - 1)
        scalar_send(it, 1, r["sc_y"], [at(d_lat=d) for d in range(1, n_lat)])

        @pl.loop(0, GROUPS)
        def _(g):
            adjoint_group(it + 1, g)

        r["sc_send"][it, 2] = scalar_sum(it, 1, r["sc_y"], n_lat - 1)
        scalar_send(it, 2, r["sc_x"], [at(d_lon=d) for d in range(1, n_lon)])

        @pl.loop(0, GROUPS)
        def _(g):
            r["ag"][g] = smoothed(it + 1, g)

        sums = scalar_sum(it, 2, r["sc_x"], n_lon - 1)
        sums = jnp.sum(sums, axis=1, keepdims=True)
        squares, energy = sums[0:1], sums[1:2]
        alpha = squares / (squares + energy)

        @pl.loop(0, GROUPS)
        def _(g):
            gradient = r["grad"][g]
            r["ctl"][g] = r["ctl"][g] - alpha * gradient[:64, :128]
            r["grad"][g] = gradient - alpha * (gradient + r["ag"][g])

    @pl.loop(0, GROUPS)
    def _(g):
        for value, out in ((r["ctl"][g], r["out_c"]), (r["grad"][g, :64, :128], r["out_g"])):
            for l in range(LEV):
                turned = pltpu.roll(value, 128 - 32 * l, 1) if l else value
                for m in range(PER):
                    out[g * PER + m, l] = turned[m * 16 : m * 16 + 16, :32]

    done = lambda ref, sem: pltpu.make_async_copy(ref, ref, sem).wait()
    done(r["h_recv"].at[0], r["hs_sem"].at[0])
    for it in range(ITERS):
        done(r["h_recv"].at[it + 1, pl.ds(0, GROUPS)], r["hs_sem"].at[it + 1])
        done(r["rs_recv"].at[it], r["rss_sem"].at[it])
        done(r["rs_recv"].at[it], r["ags_sem"].at[it])
        for stage, buffer in enumerate(("sc_m", "sc_y", "sc_x")):
            done(r[buffer].at[it], r["scs_sem"].at[it, stage])


def local(sizes, ensemble, huber, innovation, sea_mask):
    n_lon, n_lat, n_mem = sizes
    vmem, dma = pltpu.VMEM, pltpu.SemaphoreType.DMA
    shapes = {n: TABLES[n].shape[1:] if n in BY_LON + BY_LAT else TABLES[n].shape for n in NAMES}
    field = (4, FINE_X, FINE_Y)
    scratch = [
        vmem((MEMBERS // n_mem, VARS, LEV, FINE_X, FINE_Y), BF),
        vmem((VARS, *field), F32),
        vmem((VARS, *field), F32),
        *(vmem(shapes[n], BF) for n in NAMES),
        vmem((5, 256, 256), BF),
        vmem((5, 256, 256), BF),
        vmem((112, 256), F32),
        vmem((GROUPS, 112, 256), F32),
        vmem((GROUPS, 112, 256), F32),
        vmem((GROUPS, 64, 128), F32),
        vmem((LEV, GROUPS, 256, 128), BF),
        vmem((256, 512), BF),
        vmem((ITERS + 1, LEV, *field), BF),
        vmem(field, F32),
        vmem((ITERS, 3, *field), BF),
        vmem((ITERS, 3, *field), BF),
        vmem((ITERS + 1, GROUPS + 1, 6, 40, 128), BF),
        vmem((ITERS + 1, GROUPS + 1, 10, 40, 128), BF),
        vmem((ITERS, 3, 8, 128), F32),
        vmem((ITERS, n_mem - 1, 8, 128), F32),
        vmem((ITERS, n_lat - 1, 8, 128), F32),
        vmem((ITERS, n_lon - 1, 8, 128), F32),
        dma((len(NAMES) + 2,)),
        dma((GROUPS,)),
        dma((ITERS + 1,)),
        dma((ITERS + 1, GROUPS + 1)),
        dma((ITERS,)),
        dma((ITERS,)),
        dma((ITERS,)),
        dma((ITERS,)),
        dma((ITERS, 3)),
        dma((ITERS, 3)),
    ]
    out = jax.ShapeDtypeStruct((MEMBERS // n_mem, LEV, OWN_X, OWN_Y), F32)
    any_space, in_vmem = pl.BlockSpec(memory_space=pl.ANY), pl.BlockSpec(memory_space=pltpu.VMEM)
    return pl.pallas_call(
        lambda *refs: kernel(sizes, *refs),
        out_shape=(out, out),
        in_specs=[any_space, any_space, any_space, in_vmem, *([any_space] * len(NAMES))],
        out_specs=(in_vmem, in_vmem),
        scratch_shapes=scratch,
        name="assimilate",
        compiler_params=pltpu.CompilerParams(collective_id=0, has_side_effects=True, vmem_limit_bytes=60 * 2**20),
    )(ensemble, huber, innovation, sea_mask, *(jnp.asarray(TABLES[n]) for n in NAMES))


def solution(mesh):
    sizes = tuple(mesh.shape[name] for name in ("lon", "lat", "mem"))
    in_specs = (
        P("mem", None, None, "lon", "lat"),
        P(None, None, "lon", "lat"),
        P(None, None, "lon", "lat"),
        P("lon", "lat"),
    )
    out_specs = (P("mem", None, "lon", "lat"), P("mem", None, "lon", "lat"))
    return jax.shard_map(
        lambda *args: local(sizes, *args), mesh=mesh, in_specs=in_specs, out_specs=out_specs, check_vma=False
    )
```

profile of v0, /device:TPU:1, one launch (start us, length us, event | category | flops | bytes accessed | tf_op | source)
XLA Modules:
  0.0 92.4 jit_solution(13374792580310290923)
XLA Ops:
  0.6 87.8 %assimilate.1 = (f32[20,4,16,32]{3,2,1,0:T(8,128)}, f32[20,4,16,32]{3,2,1,0:T(8,128)}) custom-call(bf16[20,4,4,64,128]{4,3,2,1,0:T(8,128)(2,1)} %refs_0_.1, f32[4,4,64,128]{3,2,1,0:T(8,128)} %refs_1_.1, f32[4,4,64,128]{3,2,1,0:T(8,128)} %refs_2_.1, s32[16,32]{1,0:T(8,128)} %refs_3_.1, bf16[3,5,80,128]{3,2,1,0:T(8,128)(2,1)} %constant.34.clone.refs_4_, ...), custom_call_target="tpu_custom_call" | custom-call | tf_op jit(solution)/shard_map/assimilate/pallas_call | solution.py:532
  88.5 2.0 %copy.25 = f32[20,4,16,32]{3,2,1,0:T(8,128)} copy(f32[20,4,16,32]{3,2,1,0:T(8,128)} %get-tuple-element.4) | data formatting | bytes 327680
  90.5 2.0 %copy.26 = f32[20,4,16,32]{3,2,1,0:T(8,128)} copy(f32[20,4,16,32]{3,2,1,0:T(8,128)} %get-tuple-element.5) | data formatting | bytes 327680
where the time goes:
time: 92.7 us; the launch traced here: 92.4 us
  Pallas kernels  87.8 us (95%)
  local copies, waits for them, and re-layouts  3.97 us (4%)
    pallas_call x1, Pallas kernels, local(): pl.pallas_call(lambda *refs: kernel(sizes, *refs), out_shape=(out, out),...  87.8 us
    unnamed x2, local copies, waits for them, and re-layouts  3.97 us

commit v1 on v0

v1 whole, which is shorter than its diff:
```python
import math
import typing

import jax
import jax.numpy as jnp
import numpy as np
from jax import lax
from jax.experimental import pallas as pl
from jax.experimental.pallas import tpu as pltpu
from jax.sharding import PartitionSpec as P


MEMBERS, VARS, LEV = 80, 4, 4
ITERS = 3
GROUPS, PER = 5, 4
OWN_X, OWN_Y = 16, 32
FINE_X, FINE_Y = 64, 128
CHUNK = 16
CHUNKS = FINE_X // CHUNK
SX_WEIGHT = (1.0, 2.0, 3.0, 2.0, 1.0)
SY_WEIGHT = (1.0, 2.0, 2.0, 2.0, 1.0)
S_SCALE = 1e-4
MESH = pl.DeviceIdType.MESH
BF, F32 = jnp.bfloat16, jnp.float32


def powers(count, variant):
    where = np.arange(-9, count + 9)
    inside = np.ones(where.shape)
    if variant == 0:
        inside = (where >= 0).astype(float)
    if variant == 2:
        inside = (where < count).astype(float)
    size = where.size
    table = np.eye(size) + 2 * (np.eye(size, k=1) + np.eye(size, k=-1))
    table = inside[:, None] * table * inside[None, :]
    result = [np.diag(inside)]
    for _ in range(4):
        result.append(result[-1] @ table)
    return result


def hat(fine):
    position = (np.arange(fine) + 0.5) / 4 - 0.5
    return lambda c: np.maximum(0.0, 1 - np.abs(c - position))


def window_rows():
    own = [(m, r) for m in range(PER) for r in range(16)]
    halo = [(m, r) for m in range(PER) for r in [*range(-5, 0), *range(16, 21)]]
    return own + halo + [(-1, 0)] * 8


def a_rows():
    return [(m, r) for m in range(PER) for r in range(-1, 17)] + [(-1, 0)] * 8


def b_rows():
    top = [(m, r, 0) for m in range(PER) for r in range(-1, 9)]
    bottom = [(m, r, 0) for m in range(PER) for r in range(7, 17)]
    return top + bottom


def full_rows():
    own = b_rows()
    own = own[:40] + [(m if r > 8 else -1, r, 0) for m, r, _ in own[40:]]
    before = [(m, r - 16, -1) for m in range(PER) for r in range(7, 17)]
    after = [(m, r + 16, 1) for m in range(PER) for r in range(-1, 9)]
    return own + before + after


def window_lanes():
    own = [(l, c) for l in range(LEV) for c in range(32)]
    halo = [(l, c) for l in range(LEV) for c in [*range(-5, 0), *range(32, 37)]]
    return own + halo + [(-1, 0)] * 88


def a_lanes():
    return [(l, c) for l in range(LEV) for c in range(-1, 33)] + [(-1, 0)] * 120


def strip(cells, source):
    return [(l, c, source) for l in range(LEV) for c in cells]


def b_lanes():
    gap = [(-1, 0, 0)]
    first = strip(range(-1, 9), 0) + strip(range(9, 23), 0) + gap * 32
    right, left = strip(range(23, 33), 0), strip(range(-1, 9), 0)
    return first + right + gap * 4 + right + gap * 4 + left


def full_lanes():
    gap = [(-1, 0, 0)]
    first = strip(range(-1, 9), 0) + strip(range(9, 23), 0) + gap * 32
    before, after = strip(range(-9, 1), -1), strip(range(31, 41), 1)
    return first + before + gap * 4 + strip(range(23, 33), 0) + gap * 4 + after


def exists(source, variant):
    return not ((source == -1 and variant == 0) or (source == 1 and variant == 2))


def tables():
    wr, ar, fr = window_rows(), a_rows(), full_rows()
    wl, al, fl = window_lanes(), a_lanes(), full_lanes()
    sxf = np.zeros((3, 5, 80, 128))
    sxb = np.zeros((3, 5, 112, 256))
    for variant in range(3):
        powered = powers(OWN_X, variant)
        for k in range(5):
            for i, (m, r) in enumerate(ar):
                for j, (n, q) in enumerate(wr):
                    if m == n and m >= 0:
                        sxf[variant, k, i, j] = SX_WEIGHT[k] * powered[k][r + 9, q + 9]
            for i, (m, r) in enumerate(wr):
                for j, (n, q, source) in enumerate(fr):
                    if m == n and m >= 0 and exists(source, variant):
                        sxb[variant, k, i, j] = SX_WEIGHT[k] * powered[k][r + 9, q + 9]
    base = np.zeros((3, 5, 64, 128))
    for variant in range(3):
        powered = powers(OWN_Y, variant)
        for k in range(5):
            base[variant, k, 7:57, 7:57] = SY_WEIGHT[k] * powered[4 - k]
    alive = np.zeros((3, 256, 128))
    for variant in range(3):
        for i, (l, c, source) in enumerate(fl):
            alive[variant, i, :] = float(l >= 0 and exists(source, variant))
    pick_w, pick_a, pick_f = (np.zeros((256, 128)) for _ in range(3))
    for table, order in ((pick_w, wl), (pick_a, al), (pick_f, fl)):
        for i, item in enumerate(order):
            if item[0] >= 0:
                table[i, item[1] + 16] = 1
    level = lambda order: np.array([item[0] for item in order])
    same = lambda one, two: ((level(one)[:, None] == level(two)[None, :]) & (level(one)[:, None] >= 0)).astype(float)
    same_wa, same_fw = same(wl, al), same(fl, wl)
    weight_x, weight_y = hat(FINE_X), hat(FINE_Y)
    pxf, pxt = np.zeros((256, 128)), np.zeros((80, 256))
    for j, (m, r) in enumerate(ar):
        if m >= 0:
            pxf[m * 64 : m * 64 + 64, j] = weight_x(r)
    for j, (m, r, _) in enumerate(b_rows()):
        pxt[j, m * 64 : m * 64 + 64] = weight_x(r)
    pyf, pyt = np.zeros((256, 512)), np.zeros((512, 256))
    for j, (l, c) in enumerate(al):
        if l >= 0:
            pyf[j, l * 128 : l * 128 + 128] = weight_y(c)
    for j, (l, c, _) in enumerate(b_lanes()):
        if l >= 0:
            pyt[l * 128 : l * 128 + 128, j] = weight_y(c)
    mask_x, mask_y = np.zeros((80, 16)), np.zeros((32, 256))
    for i, (m, r, _) in enumerate(b_rows()):
        if 0 <= r < 16:
            mask_x[i, r] = 1
    for j, (l, c, _) in enumerate(b_lanes()):
        if l >= 0 and 0 <= c < 32:
            mask_y[c, j] = 1
    home = lambda value, count: -1 if value < 0 else (1 if value >= count else 0)
    take_x, take_y = np.zeros((112, 256)), np.zeros((256, 256))
    for i, (m, r) in enumerate(wr):
        for j, (n, q, source) in enumerate(fr):
            if m == n and m >= 0 and r == q and source == home(r, 16):
                take_x[i, j] = 1
    for j, (l, c) in enumerate(wl):
        for i, (n, q, source) in enumerate(fl):
            if l == n and l >= 0 and c == q and source == home(c, 32):
                take_y[i, j] = 1
    named = dict(
        sxf=sxf, sxb=sxb, base=base, alive=alive, pick_w=pick_w, pick_a=pick_a, pick_f=pick_f, same_wa=same_wa,
        same_fw=same_fw, pxf=pxf, pxt=pxt, pyf=pyf, pyt=pyt, mask_x=mask_x, mask_y=mask_y, take_x=take_x, take_y=take_y,
    )
    named.update(sxf=sxf.reshape(3, 400, 128), sxb=sxb.reshape(3, 560, 256))
    return {name: np.asarray(value, np.float32).astype(BF) for name, value in named.items()}


TABLES = tables()
NAMES = tuple(TABLES)
BY_LON, BY_LAT = ("sxf", "sxb"), ("base", "alive")


def dot(a, b):
    return lax.dot_general(a, b, (((1,), (0,)), ((), ())), preferred_element_type=F32)


def dot_nt(a, b):
    return lax.dot_general(a, b, (((1,), (1,)), ((), ())), preferred_element_type=F32)


class Refs(typing.NamedTuple):
    ens_hbm: typing.Any
    hub_hbm: typing.Any
    inn_hbm: typing.Any
    mask_ref: typing.Any
    sxf_hbm: typing.Any
    sxb_hbm: typing.Any
    base_hbm: typing.Any
    alive_hbm: typing.Any
    pick_w_hbm: typing.Any
    pick_a_hbm: typing.Any
    pick_f_hbm: typing.Any
    same_wa_hbm: typing.Any
    same_fw_hbm: typing.Any
    pxf_hbm: typing.Any
    pxt_hbm: typing.Any
    pyf_hbm: typing.Any
    pyt_hbm: typing.Any
    mask_x_hbm: typing.Any
    mask_y_hbm: typing.Any
    take_x_hbm: typing.Any
    take_y_hbm: typing.Any
    out_c: typing.Any
    out_g: typing.Any
    ens: typing.Any
    hub: typing.Any
    inn: typing.Any
    sxf: typing.Any
    sxb: typing.Any
    base: typing.Any
    alive: typing.Any
    pick_w: typing.Any
    pick_a: typing.Any
    pick_f: typing.Any
    same_wa: typing.Any
    same_fw: typing.Any
    pxf: typing.Any
    pxt: typing.Any
    pyf: typing.Any
    pyt: typing.Any
    mask_x: typing.Any
    mask_y: typing.Any
    take_x: typing.Any
    take_y: typing.Any
    syf: typing.Any
    syb: typing.Any
    win_mask: typing.Any
    grad: typing.Any
    ag: typing.Any
    ctl: typing.Any
    u_fwd: typing.Any
    u_back: typing.Any
    coarse: typing.Any
    fine: typing.Any
    wbuf: typing.Any
    spread: typing.Any
    mis: typing.Any
    rs_own: typing.Any
    rs_send: typing.Any
    rs_recv: typing.Any
    h_send: typing.Any
    h_recv: typing.Any
    d_send: typing.Any
    d_recv: typing.Any
    sc_send: typing.Any
    sc_a: typing.Any
    sc_b: typing.Any
    in_sem: typing.Any
    ens_sem: typing.Any
    hs_sem: typing.Any
    hr_sem: typing.Any
    ds_sem: typing.Any
    dr_sem: typing.Any
    rss_sem: typing.Any
    rsr_sem: typing.Any
    ags_sem: typing.Any
    agr_sem: typing.Any
    scs_sem: typing.Any
    scr_sem: typing.Any


def kernel(sizes, *refs):
    n_lon, n_lat, n_mem = sizes
    r = Refs(*refs)
    lon, lat, mem = lax.axis_index("lon"), lax.axis_index("lat"), lax.axis_index("mem")
    scale = 1.0 / math.sqrt(MEMBERS - 1)

    def at(d_lon=0, d_lat=0, d_mem=0):
        return {
            "lon": lax.rem(lon + (d_lon + n_lon), n_lon),
            "lat": lax.rem(lat + (d_lat + n_lat), n_lat),
            "mem": lax.rem(mem + (d_mem + n_mem), n_mem),
        }

    def wait(ref, sem):
        pltpu.make_async_copy(ref, ref, sem).wait()

    def send(source, target, send_sem, recv_sem, device):
        pltpu.make_async_remote_copy(
            src_ref=source, dst_ref=target, send_sem=send_sem, recv_sem=recv_sem, device_id=device, device_id_type=MESH
        ).start()

    variant_x = jnp.where(lon == 0, 0, jnp.where(lon == n_lon - 1, 2, 1))
    variant_y = jnp.where(lat == 0, 0, jnp.where(lat == n_lat - 1, 2, 1))
    loads = {}
    first = ["hub", "inn", "mask_x", "mask_y", "pxt", "pyt"]
    order = [*first, *(n for n in NAMES if n not in first)]

    def load(i):
        name = order[i]
        source = getattr(r, name + "_hbm")
        if name in BY_LON:
            source = source.at[variant_x]
        if name in BY_LAT:
            source = source.at[variant_y]
        loads[name] = pltpu.make_async_copy(source, getattr(r, name), r.in_sem.at[i])
        loads[name].start()

    for i in range(len(first)):
        load(i)
    for g in range(GROUPS):
        part = pl.ds(g * PER, PER)
        pltpu.make_async_copy(r.ens_hbm.at[part], r.ens.at[part], r.ens_sem.at[g]).start()
    for i in range(len(first), len(order)):
        load(i)

    barrier = pltpu.get_barrier_semaphore()
    plane = [at(d_lat=dy, d_mem=dm) for dy in range(n_lat) for dm in range(n_mem) if dy or dm]
    line = [at(d_lon=d) for d in range(1, n_lon)]
    partners = plane + line + [at(d_lon=dx, d_lat=dy) for dx in (-1, 1) for dy in (-1, 1)]
    for partner in partners:
        pl.semaphore_signal(barrier, inc=1, device_id=partner, device_id_type=MESH)

    lane = lax.broadcasted_iota(jnp.int32, (40, 128), 1)
    low = lane[:24] < 64

    for name in first:
        loads[name].wait()

    @pl.loop(0, CHUNKS)
    def _(c):
        rows = pl.ds(pl.multiple_of(c * CHUNK, CHUNK), CHUNK)
        for l in range(LEV):
            for v in range(VARS):
                r.mis[0, c, l, v] = (r.hub[v, l, rows] * r.inn[v, l, rows]).astype(BF)

    with jax.named_scope("w_bar"):
        pl.semaphore_wait(barrier, len(partners))

    def send_strips(e, g, b):
        first, second = b[:, :128], b[:, 128:]
        top, bottom = second[:40], second[40:]
        turned, turned_top = pltpu.roll(bottom, 64, 1), pltpu.roll(top[16:], 64, 1)
        out, corner = r.h_send.at[e, g], r.d_send.at[e, g]
        out[0] = first[:40].astype(BF)
        out[1] = top.astype(BF)
        out[2] = first[40:].astype(BF)
        out[3] = bottom.astype(BF)
        out[4] = jnp.where(lane < 64, turned, top).astype(BF)
        out[5] = jnp.where(lane < 64, top, turned).astype(BF)
        corner[0] = jnp.where(low, turned_top, top[:24]).astype(BF)
        corner[1] = jnp.where(low, top[:24], turned_top).astype(BF)
        corner[2] = jnp.where(low, turned[16:], bottom[:24]).astype(BF)
        corner[3] = jnp.where(low, bottom[:24], turned[16:]).astype(BF)
        strips = ((4, 1, 5, (0, -1)), (5, 1, 4, (0, 1)), (0, 2, 2, (-1, 0)), (2, 2, 0, (1, 0)))
        corners = ((0, 3, (-1, -1)), (1, 2, (-1, 1)), (2, 1, (1, -1)), (3, 0, (1, 1)))
        for source, target, (dx, dy) in corners:
            send(
                r.d_send.at[e, g, source], r.d_recv.at[e, g, target],
                r.ds_sem.at[e], r.dr_sem.at[e, g], at(d_lon=dx, d_lat=dy),
            )
        for source, count, target, (dx, dy) in strips:
            send(
                r.h_send.at[e, g, pl.ds(source, count)], r.h_recv.at[e, g, pl.ds(target, count)],
                r.hs_sem.at[e], r.hr_sem.at[e, g], at(d_lon=dx, d_lat=dy),
            )

    def spread_rows(e, c, g):
        for l in range(LEV):
            weights = [r.mis[e, c, l, v].astype(F32) for v in range(VARS)]
            rows = pl.ds(pl.multiple_of(c * CHUNK, CHUNK), CHUNK)
            for m in range(PER):
                total = sum(r.ens[g * PER + m, v, l, rows].astype(F32) * weights[v] for v in range(VARS))
                place = pl.ds(pl.multiple_of(m * 64 + c * CHUNK, CHUNK), CHUNK)
                r.spread[g, place, l * 128 : l * 128 + 128] = total.astype(BF)

    def coarse_send(e, g):
        rows = dot(r.pxt[...], r.spread[g]).astype(BF)
        send_strips(e, g, dot(rows, r.pyt[...]) * scale)

    def assembled(e, g):
        with jax.named_scope("w_halo"):
            wait(r.h_recv.at[e, g], r.hr_sem.at[e, g])
            wait(r.d_recv.at[e, g], r.dr_sem.at[e, g])
        own = [r.h_send[e, g, i].astype(F32) for i in range(4)]
        got = [r.h_recv[e, g, i].astype(F32) for i in range(6)]
        corner = [r.d_recv[e, g, i].astype(F32) for i in range(4)]
        corner = [jnp.concatenate([d, pltpu.roll(d[8:], 64, 1)], axis=0) for d in corner]

        def second(before, middle, after):
            return jnp.where(lane < 42, before, jnp.where(lane < 86, middle, after))

        first = jnp.concatenate([own[0], own[2], got[0], got[2]], axis=0)
        other = jnp.concatenate(
            [
                second(got[4], own[1], got[5]),
                second(pltpu.roll(got[4], 64, 1), own[3], pltpu.roll(got[5], 64, 1)),
                second(corner[0], got[1], corner[1]),
                second(corner[2], got[3], corner[3]),
            ],
            axis=0,
        )
        return jnp.concatenate([first, other], axis=1).astype(BF)

    def smoothed(e, store):
        for g in range(GROUPS):
            part = dot(r.sxb[:, :160], assembled(e, g))
            for k in range(5):
                r.u_back[k, g * 112 : g * 112 + 112] = part[k * 112 : k * 112 + 112].astype(BF)
        total = dot(r.u_back[0], r.syb[0])
        for k in range(1, 5):
            total = total + dot(r.u_back[k], r.syb[k])
        for g in range(GROUPS):
            store(g, total[g * 112 : g * 112 + 112] * r.win_mask[...])

    mask = r.mask_ref[...].astype(F32).astype(BF)
    mask_rows = dot(r.mask_x[...], mask).astype(BF)
    send_strips(0, GROUPS, dot(mask_rows, r.mask_y[...]))

    @pl.loop(0, GROUPS)
    def _(g):
        part = pl.ds(g * PER, PER)
        with jax.named_scope("w_ens"):
            pltpu.make_async_copy(r.ens_hbm.at[part], r.ens.at[part], r.ens_sem.at[g]).wait()
        with jax.named_scope("adj0"):
            for c in range(CHUNKS):
                spread_rows(0, c, g)
            coarse_send(0, g)

    for name in order:
        if name not in first:
            loads[name].wait()

    @pl.loop(0, 5)
    @jax.named_scope("expand")
    def _(k):
        base = r.base[k]
        base = jnp.concatenate([base, jnp.zeros_like(base)], axis=0)
        to_a = dot_nt(base, r.pick_a[...]).astype(BF)
        to_w = dot_nt(base, r.pick_w[...]).astype(BF)
        r.syf[k] = (dot(r.pick_w[...], to_a).astype(BF) * r.same_wa[...]).astype(BF)
        spread_f = dot(r.pick_f[...] * r.alive[...], to_w).astype(BF)
        r.syb[k] = (spread_f * r.same_fw[...]).astype(BF)

    picked = dot(r.take_x[:, :160], assembled(0, GROUPS)).astype(BF)
    r.win_mask[...] = dot(picked, r.take_y[...]) * S_SCALE

    def store_first(g, value):
        r.grad[g] = -value
        r.ctl[g] = jnp.zeros((64, 128), F32)

    with jax.named_scope("post0"):
        smoothed(0, store_first)

    row8 = lax.broadcasted_iota(jnp.int32, (8, 128), 0)

    def scalar_send(it, stage, buffer, targets):
        for slot, target in enumerate(targets):
            send(
                r.sc_send.at[it, stage], buffer.at[it, slot], r.scs_sem.at[it, stage], r.scr_sem.at[it, stage], target
            )

    def scalar_sum(it, stage, buffer, count):
        with jax.named_scope("w_sc"):
            wait(buffer.at[it], r.scr_sem.at[it, stage])
        total = r.sc_send[it, stage]
        for slot in range(count):
            total = total + buffer[it, slot]
        return total

    @pl.loop(0, ITERS)
    def _(it):
        with jax.named_scope("fine"):
            squares = jnp.zeros((8, 128), F32)
            for g in range(GROUPS):
                own = r.grad[g, :64, :128]
                squares = squares + jnp.sum((own * own).reshape(8, 8, 128), axis=0)
                part = dot(r.sxf[:, :112], r.grad[g].astype(BF))
                for k in range(5):
                    r.u_fwd[k, g * 80 : g * 80 + 80] = part[k * 80 : k * 80 + 80].astype(BF)
            total = dot(r.u_fwd[0], r.syf[0])
            for k in range(1, 5):
                total = total + dot(r.u_fwd[k], r.syf[k])
            r.coarse[...] = (total * S_SCALE).astype(BF)
            r.fine[...] = dot(r.coarse[...], r.pyf[...]).astype(BF)
            for g in range(GROUPS):
                part = dot(r.pxf[:, :80], r.fine[g * 80 : g * 80 + 80]).astype(BF)
                for l in range(LEV):
                    r.wbuf[l, g] = part[:, l * 128 : l * 128 + 128]

        @pl.loop(0, CHUNKS)
        @jax.named_scope("inc")
        def _(c):
            start = pl.multiple_of(c * CHUNK, CHUNK)
            rows = pl.ds(start, CHUNK)
            for step, away in enumerate((2, 1, 3, 0)):
                level = lax.rem(mem + away, n_mem)
                sums = [jnp.zeros((CHUNK, 128), F32) for _ in range(VARS)]
                for m in range(GROUPS * PER):
                    place = pl.ds(pl.multiple_of((m % PER) * 64 + start, CHUNK), CHUNK)
                    weight = r.wbuf[level, m // PER, place].astype(F32)
                    for v in range(VARS):
                        sums[v] = sums[v] + r.ens[m, v, level, rows].astype(F32) * weight
                for v in range(VARS):
                    if away:
                        r.rs_send[it, c, step, v] = sums[v].astype(BF)
                    else:
                        r.rs_own[c, v] = sums[v]
                if away:
                    send(
                        r.rs_send.at[it, c, step], r.rs_recv.at[it, c, step],
                        r.rss_sem.at[it], r.rsr_sem.at[it, c], at(d_mem=away),
                    )

        def misfit_rows(c, energy):
            with jax.named_scope("w_rs"):
                wait(r.rs_recv.at[it, c], r.rsr_sem.at[it, c])
            rows = pl.ds(pl.multiple_of(c * CHUNK, CHUNK), CHUNK)
            for v in range(VARS):
                total = r.rs_own[c, v]
                for step in range(3):
                    total = total + r.rs_recv[it, c, step, v].astype(F32)
                total = total * scale
                rounded = (r.hub[v, mem, rows] * total).astype(BF)
                r.mis[it + 1, c, mem, v] = rounded
                product = rounded.astype(F32) * total
                energy = energy + product[:8] + product[8:]
            for away in (2, 1, 3):
                send(
                    r.mis.at[it + 1, c, mem], r.mis.at[it + 1, c, mem],
                    r.ags_sem.at[it], r.agr_sem.at[it, c], at(d_mem=away),
                )
            return energy

        energy = lax.fori_loop(0, CHUNKS, misfit_rows, jnp.zeros((8, 128), F32))
        squares = jnp.sum(squares, axis=0, keepdims=True)
        energy = jnp.sum(energy, axis=0, keepdims=True)
        r.sc_send[it, 0] = jnp.where(row8 == 0, squares, jnp.where(row8 == 1, energy, 0.0))
        scalar_send(it, 0, r.sc_a, plane)

        @pl.loop(0, CHUNKS - 1)
        def _(c):
            with jax.named_scope("w_ag"):
                wait(r.rs_recv.at[it, c], r.agr_sem.at[it, c])

            with jax.named_scope("adj"):
                @pl.loop(0, GROUPS)
                def _(g):
                    spread_rows(it + 1, c, g)

        with jax.named_scope("w_ag"):
            wait(r.rs_recv.at[it, CHUNKS - 1], r.agr_sem.at[it, CHUNKS - 1])

        with jax.named_scope("adj_send"):
            for g in range(GROUPS):
                spread_rows(it + 1, CHUNKS - 1, g)
                coarse_send(it + 1, g)

        r.sc_send[it, 1] = scalar_sum(it, 0, r.sc_a, len(plane))
        scalar_send(it, 1, r.sc_b, line)

        def store_image(g, value):
            r.ag[g] = value

        with jax.named_scope("post"):
            smoothed(it + 1, store_image)

        sums = scalar_sum(it, 1, r.sc_b, len(line))
        sums = jnp.sum(sums, axis=1, keepdims=True)
        squares, energy = sums[0:1], sums[1:2]
        alpha = squares / (squares + energy)

        with jax.named_scope("upd"):
            for g in range(GROUPS):
                gradient = r.grad[g]
                r.ctl[g] = r.ctl[g] - alpha * gradient[:64, :128]
                r.grad[g] = gradient - alpha * (gradient + r.ag[g])

    for g in range(GROUPS):
        r.out_c[g] = r.ctl[g]
        r.out_g[g] = r.grad[g, :64, :128]

    wait(r.h_recv.at[0], r.hs_sem.at[0])
    wait(r.d_recv.at[0], r.ds_sem.at[0])
    for it in range(ITERS):
        wait(r.h_recv.at[it + 1, pl.ds(0, GROUPS)], r.hs_sem.at[it + 1])
        wait(r.d_recv.at[it + 1, pl.ds(0, GROUPS)], r.ds_sem.at[it + 1])
        wait(r.rs_recv.at[it], r.rss_sem.at[it])
        wait(r.rs_recv.at[it], r.ags_sem.at[it])
        wait(r.sc_a.at[it], r.scs_sem.at[it, 0])
        wait(r.sc_b.at[it], r.scs_sem.at[it, 1])


def unpack(*refs):
    for source, out in (refs[0::2], refs[1::2]):
        for g in range(GROUPS):
            for l in range(LEV):
                turned = pltpu.roll(source[g], 128 - 32 * l, 1) if l else source[g]
                for m in range(PER):
                    out[g * PER + m, l] = turned[m * 16 : m * 16 + 16, :32]


def local(sizes, ensemble, huber, innovation, sea_mask):
    n_lon, n_lat, n_mem = sizes
    vmem, dma = pltpu.VMEM, pltpu.SemaphoreType.DMA
    shapes = {n: TABLES[n].shape[1:] if n in BY_LON + BY_LAT else TABLES[n].shape for n in NAMES}
    field = (VARS, FINE_X, FINE_Y)
    rows = (VARS, CHUNK, FINE_Y)
    times = ITERS + 1
    scratch = [
        vmem((MEMBERS // n_mem, VARS, LEV, FINE_X, FINE_Y), BF),
        vmem((LEV, *field), F32),
        vmem((LEV, *field), F32),
        *(vmem(shapes[n], BF) for n in NAMES),
        vmem((5, 256, 256), BF),
        vmem((5, 256, 256), BF),
        vmem((112, 256), F32),
        vmem((GROUPS, 112, 256), F32),
        vmem((GROUPS, 112, 256), F32),
        vmem((GROUPS, 64, 128), F32),
        vmem((5, GROUPS * 80, 256), BF),
        vmem((5, GROUPS * 112, 256), BF),
        vmem((GROUPS * 80, 256), BF),
        vmem((GROUPS * 80, 512), BF),
        vmem((LEV, GROUPS, 256, 128), BF),
        vmem((GROUPS, 256, 512), BF),
        vmem((times, CHUNKS, LEV, *rows), BF),
        vmem((CHUNKS, *rows), F32),
        vmem((ITERS, CHUNKS, 3, *rows), BF),
        vmem((ITERS, CHUNKS, 3, *rows), BF),
        vmem((times, GROUPS + 1, 6, 40, 128), BF),
        vmem((times, GROUPS + 1, 6, 40, 128), BF),
        vmem((times, GROUPS + 1, 4, 24, 128), BF),
        vmem((times, GROUPS + 1, 4, 24, 128), BF),
        vmem((ITERS, 2, 8, 128), F32),
        vmem((ITERS, n_mem * n_lat - 1, 8, 128), F32),
        vmem((ITERS, n_lon - 1, 8, 128), F32),
        dma((len(NAMES) + 2,)),
        dma((GROUPS,)),
        dma((times,)),
        dma((times, GROUPS + 1)),
        dma((times,)),
        dma((times, GROUPS + 1)),
        dma((ITERS,)),
        dma((ITERS, CHUNKS)),
        dma((ITERS,)),
        dma((ITERS, CHUNKS)),
        dma((ITERS, 2)),
        dma((ITERS, 2)),
    ]
    packed = jax.ShapeDtypeStruct((GROUPS, PER * OWN_X, 128), F32)
    any_space, in_vmem = pl.BlockSpec(memory_space=pl.ANY), pl.BlockSpec(memory_space=pltpu.VMEM)
    control, gradient = pl.pallas_call(
        lambda *refs: kernel(sizes, *refs),
        out_shape=(packed, packed),
        in_specs=[any_space, any_space, any_space, in_vmem, *([any_space] * len(NAMES))],
        out_specs=(in_vmem, in_vmem),
        scratch_shapes=scratch,
        name="assimilate",
        compiler_params=pltpu.CompilerParams(collective_id=0, has_side_effects=True, vmem_limit_bytes=60 * 2**20),
    )(ensemble, huber, innovation, sea_mask, *(jnp.asarray(TABLES[n]) for n in NAMES))
    out = jax.ShapeDtypeStruct((MEMBERS // n_mem, LEV, OWN_X, OWN_Y), F32)
    return pl.pallas_call(
        unpack, out_shape=(out, out), in_specs=[in_vmem] * 2, out_specs=(in_vmem, in_vmem), name="unpack"
    )(control, gradient)


def solution(mesh):
    sizes = tuple(mesh.shape[name] for name in ("lon", "lat", "mem"))
    in_specs = (
        P("mem", None, None, "lon", "lat"),
        P(None, None, "lon", "lat"),
        P(None, None, "lon", "lat"),
        P("lon", "lat"),
    )
    out_specs = (P("mem", None, "lon", "lat"), P("mem", None, "lon", "lat"))
    return jax.shard_map(
        lambda *args: local(sizes, *args), mesh=mesh, in_specs=in_specs, out_specs=out_specs, check_vma=False
    )
```

time: 92.7 us -> 75.1 us (0.81)
  Pallas kernels: 87.8 us -> 74.3 us
  local copies, waits for them, and re-layouts: 3.97 us -> 0 us
    pallas_call x1 -> x2, Pallas kernels: 87.8 us -> 74.3 us  [the longest x1 72 us: local(): pl.pallas_call(lambda *refs: kernel(sizes, *refs), out_shape=(packed, pac...]
    unnamed x2 -> x0, local copies, waits for them, and re-layouts: 3.97 us -> none
where the time goes in v1:
time: 75.1 us; the launch traced here: 74.9 us
  Pallas kernels  74.3 us (99%)
    pallas_call x1, Pallas kernels, local(): pl.pallas_call(lambda *refs: kernel(sizes, *refs), out_shape=(packed, pac...  72 us
    pallas_call x1, Pallas kernels, local(): pl.pallas_call(unpack, out_shape=(out, out), in_specs=[in_vmem] * 2, out_...  2.3 us

profile of v1, /device:TPU:1, one launch (start us, length us, event | category | flops | bytes accessed | tf_op | source)
XLA Modules:
  0.0 74.9 jit_solution(17890188568543871936)
XLA Ops:
  0.6 72.0 %assimilate.1 = (f32[5,64,128]{2,1,0:T(8,128)}, f32[5,64,128]{2,1,0:T(8,128)}) custom-call(bf16[20,4,4,64,128]{4,3,2,1,0:T(8,128)(2,1)} %refs_0_.1, f32[4,4,64,128]{3,2,1,0:T(8,128)} %refs_1_.1, f32[4,4,64,128]{3,2,1,0:T(8,128)} %refs_2_.1, s32[16,32]{1,0:T(8,128)} %refs_3_.1, bf16[3,400,128]{2,1,0:T(8,128)(2,1)} %constant.34.clone.refs_4_, ...), custom_call_target="tpu_custom_call" | custom-call | tf_op jit(solution)/shard_map/assimilate/pallas_call | solution.py:651
  72.6 2.3 %unpack.1 = (f32[20,4,16,32]{3,2,1,0:T(8,128)}, f32[20,4,16,32]{3,2,1,0:T(8,128)}) custom-call(f32[5,64,128]{2,1,0:T(8,128)} %get-tuple-element.4.refs_0_, f32[5,64,128]{2,1,0:T(8,128)} %get-tuple-element.5.refs_1_), custom_call_target="tpu_custom_call" | custom-call | tf_op jit(solution)/shard_map/unpack/pallas_call | solution.py:661

commit v2 on v1

--- a/solution.py
+++ b/solution.py
@@ -13,6 +13,7 @@
 MEMBERS, VARS, LEV = 80, 4, 4
 ITERS = 3
 GROUPS, PER = 5, 4
+BATCHES = ((0, 1, 2), (3, 4))
 OWN_X, OWN_Y = 16, 32
 FINE_X, FINE_Y = 64, 128
 CHUNK = 16
@@ -117,11 +118,11 @@
                 for j, (n, q, source) in enumerate(fr):
                     if m == n and m >= 0 and exists(source, variant):
                         sxb[variant, k, i, j] = SX_WEIGHT[k] * powered[k][r + 9, q + 9]
-    base = np.zeros((3, 5, 64, 128))
+    base = np.zeros((3, 320, 128))
     for variant in range(3):
         powered = powers(OWN_Y, variant)
         for k in range(5):
-            base[variant, k, 7:57, 7:57] = SY_WEIGHT[k] * powered[4 - k]
+            base[variant, k * 64 + 7 : k * 64 + 57, 7:57] = SY_WEIGHT[k] * powered[4 - k]
     alive = np.zeros((3, 256, 128))
     for variant in range(3):
         for i, (l, c, source) in enumerate(fl):
@@ -176,6 +177,7 @@
 TABLES = tables()
 NAMES = tuple(TABLES)
 BY_LON, BY_LAT = ("sxf", "sxb"), ("base", "alive")
+SPREAD_TABLES = ("base", "alive", "pick_w", "pick_a", "pick_f", "same_wa", "same_fw")
 
 
 def dot(a, b):
@@ -190,7 +192,7 @@
     ens_hbm: typing.Any
     hub_hbm: typing.Any
     inn_hbm: typing.Any
-    mask_ref: typing.Any
+    mask_hbm: typing.Any
     sxf_hbm: typing.Any
     sxb_hbm: typing.Any
     base_hbm: typing.Any
@@ -213,6 +215,7 @@
     ens: typing.Any
     hub: typing.Any
     inn: typing.Any
+    mask: typing.Any
     sxf: typing.Any
     sxb: typing.Any
     base: typing.Any
@@ -242,12 +245,15 @@
     fine: typing.Any
     wbuf: typing.Any
     spread: typing.Any
+    rows: typing.Any
     mis: typing.Any
     rs_own: typing.Any
     rs_send: typing.Any
     rs_recv: typing.Any
     h_send: typing.Any
     h_recv: typing.Any
+    l_send: typing.Any
+    l_recv: typing.Any
     d_send: typing.Any
     d_recv: typing.Any
     sc_send: typing.Any
@@ -257,6 +263,8 @@
     ens_sem: typing.Any
     hs_sem: typing.Any
     hr_sem: typing.Any
+    ls_sem: typing.Any
+    lr_sem: typing.Any
     ds_sem: typing.Any
     dr_sem: typing.Any
     rss_sem: typing.Any
@@ -291,8 +299,9 @@
     variant_x = jnp.where(lon == 0, 0, jnp.where(lon == n_lon - 1, 2, 1))
     variant_y = jnp.where(lat == 0, 0, jnp.where(lat == n_lat - 1, 2, 1))
     loads = {}
-    first = ["hub", "inn", "mask_x", "mask_y", "pxt", "pyt"]
-    order = [*first, *(n for n in NAMES if n not in first)]
+    early = [n for n in NAMES if n in SPREAD_TABLES]
+    first = ["hub", "inn", "mask", "mask_x", "mask_y", "pxt", "pyt"]
+    order = [*early, *first, *(n for n in NAMES if n not in [*early, *first])]
 
     def load(i):
         name = order[i]
@@ -304,12 +313,13 @@
         loads[name] = pltpu.make_async_copy(source, getattr(r, name), r.in_sem.at[i])
         loads[name].start()
 
-    for i in range(len(first)):
+    ready = len(early) + len(first)
+    for i in range(ready):
         load(i)
     for g in range(GROUPS):
         part = pl.ds(g * PER, PER)
         pltpu.make_async_copy(r.ens_hbm.at[part], r.ens.at[part], r.ens_sem.at[g]).start()
-    for i in range(len(first), len(order)):
+    for i in range(ready, len(order)):
         load(i)
 
     barrier = pltpu.get_barrier_semaphore()
@@ -320,7 +330,16 @@
         pl.semaphore_signal(barrier, inc=1, device_id=partner, device_id_type=MESH)
 
     lane = lax.broadcasted_iota(jnp.int32, (40, 128), 1)
-    low = lane[:24] < 64
+    for name in early:
+        loads[name].wait()
+
+    with jax.named_scope("expand"):
+        to_a = dot_nt(r.base[...], r.pick_a[...]).astype(BF)
+        to_w = dot_nt(r.base[...], r.pick_w[...]).astype(BF)
+        for k in range(5):
+            rows = slice(k * 64, k * 64 + 64)
+            r.syf[k] = dot(r.pick_w[:, :64], to_a[rows]).astype(BF) * r.same_wa[...]
+            r.syb[k] = dot(r.pick_f[:, :64] * r.alive[:, :64], to_w[rows]).astype(BF) * r.same_fw[...]
 
     for name in first:
         loads[name].wait()
@@ -335,32 +354,37 @@
     with jax.named_scope("w_bar"):
         pl.semaphore_wait(barrier, len(partners))
 
-    def send_strips(e, g, b):
+    def three(one, two, last, turns):
+        one, two, last = (pltpu.roll(x, t, 1) if t else x for x, t in zip((one, two, last), turns))
+        at_lane = lane[: one.shape[0]]
+        return jnp.where(at_lane < 42, one, jnp.where(at_lane < 86, two, last)).astype(BF)
+
+    def pack_strips(e, g, b):
         first, second = b[:, :128], b[:, 128:]
-        top, bottom = second[:40], second[40:]
-        turned, turned_top = pltpu.roll(bottom, 64, 1), pltpu.roll(top[16:], 64, 1)
-        out, corner = r.h_send.at[e, g], r.d_send.at[e, g]
+        out, lats, corner = r.h_send.at[e, g], r.l_send.at[e, g], r.d_send.at[e, g]
         out[0] = first[:40].astype(BF)
-        out[1] = top.astype(BF)
+        out[1] = second[:40].astype(BF)
         out[2] = first[40:].astype(BF)
-        out[3] = bottom.astype(BF)
-        out[4] = jnp.where(lane < 64, turned, top).astype(BF)
-        out[5] = jnp.where(lane < 64, top, turned).astype(BF)
-        corner[0] = jnp.where(low, turned_top, top[:24]).astype(BF)
-        corner[1] = jnp.where(low, top[:24], turned_top).astype(BF)
-        corner[2] = jnp.where(low, turned[16:], bottom[:24]).astype(BF)
-        corner[3] = jnp.where(low, bottom[:24], turned[16:]).astype(BF)
-        strips = ((4, 1, 5, (0, -1)), (5, 1, 4, (0, 1)), (0, 2, 2, (-1, 0)), (2, 2, 0, (1, 0)))
-        corners = ((0, 3, (-1, -1)), (1, 2, (-1, 1)), (2, 1, (1, -1)), (3, 0, (1, 1)))
-        for source, target, (dx, dy) in corners:
+        out[3] = second[40:].astype(BF)
+        for side, turns in enumerate(((40, 84, 0), (0, 44, 88))):
+            lats[side] = three(second[:32], second[24:56], second[48:], turns)
+            corner[side] = three(second[:16], second[16:32], second[24:40], turns)
+            corner[2 + side] = three(second[40:56], second[56:72], second[64:], turns)
+
+    def send_strips(e, g):
+        for source, target, (dx, dy) in ((0, 3, (-1, -1)), (1, 2, (-1, 1)), (2, 1, (1, -1)), (3, 0, (1, 1))):
             send(
                 r.d_send.at[e, g, source], r.d_recv.at[e, g, target],
                 r.ds_sem.at[e], r.dr_sem.at[e, g], at(d_lon=dx, d_lat=dy),
             )
-        for source, count, target, (dx, dy) in strips:
+        for side, dy in ((0, -1), (1, 1)):
             send(
-                r.h_send.at[e, g, pl.ds(source, count)], r.h_recv.at[e, g, pl.ds(target, count)],
-                r.hs_sem.at[e], r.hr_sem.at[e, g], at(d_lon=dx, d_lat=dy),
+                r.l_send.at[e, g, side], r.l_recv.at[e, g, side], r.ls_sem.at[e], r.lr_sem.at[e, g], at(d_lat=dy)
+            )
+        for source, target, dx in ((0, 2, -1), (2, 0, 1)):
+            send(
+                r.h_send.at[e, g, pl.ds(source, 2)], r.h_recv.at[e, g, pl.ds(target, 2)],
+                r.hs_sem.at[e], r.hr_sem.at[e, g], at(d_lon=dx),
             )
 
     def spread_rows(e, c, g):
@@ -372,73 +396,90 @@
                 place = pl.ds(pl.multiple_of(m * 64 + c * CHUNK, CHUNK), CHUNK)
                 r.spread[g, place, l * 128 : l * 128 + 128] = total.astype(BF)
 
-    def coarse_send(e, g):
-        rows = dot(r.pxt[...], r.spread[g]).astype(BF)
-        send_strips(e, g, dot(rows, r.pyt[...]) * scale)
-
-    def assembled(e, g):
+    def coarse_rows(e, g):
+        r.rows[g * 80 : g * 80 + 80] = dot(r.pxt[...], r.spread[g]).astype(BF)
+
+    def coarse_send(e, groups):
+        low, high = groups[0] * 80, groups[-1] * 80 + 80
+        total = dot(r.rows[low:high], r.pyt[...]) * scale
+        for i, g in enumerate(groups):
+            pack_strips(e, g, total[i * 80 : i * 80 + 80])
+        for g in groups:
+            send_strips(e, g)
+
+    def arrived(e, g):
         with jax.named_scope("w_halo"):
             wait(r.h_recv.at[e, g], r.hr_sem.at[e, g])
+            wait(r.l_recv.at[e, g], r.lr_sem.at[e, g])
             wait(r.d_recv.at[e, g], r.dr_sem.at[e, g])
+
+    def assembled(e, g):
         own = [r.h_send[e, g, i].astype(F32) for i in range(4)]
-        got = [r.h_recv[e, g, i].astype(F32) for i in range(6)]
+        got = [r.h_recv[e, g, i].astype(F32) for i in range(4)]
+        left, right = r.l_recv[e, g, 0].astype(F32), r.l_recv[e, g, 1].astype(F32)
         corner = [r.d_recv[e, g, i].astype(F32) for i in range(4)]
-        corner = [jnp.concatenate([d, pltpu.roll(d[8:], 64, 1)], axis=0) for d in corner]
+        turn = lambda x, t: pltpu.roll(x, t, 1)
 
         def second(before, middle, after):
+            before, after = jnp.concatenate(before, axis=0), jnp.concatenate(after, axis=0)
             return jnp.where(lane < 42, before, jnp.where(lane < 86, middle, after))
 
+        left_one, left_two = turn(left, 88), turn(left, 44)
+        right_two, right_last = turn(right, 84), turn(right, 40)
+        from_left = lambda x: [turn(x, 88), turn(x, 44), x[8:]]
+        from_right = lambda x: [x, turn(x, 84), turn(x, 40)[8:]]
         first = jnp.concatenate([own[0], own[2], got[0], got[2]], axis=0)
         other = jnp.concatenate(
             [
-                second(got[4], own[1], got[5]),
-                second(pltpu.roll(got[4], 64, 1), own[3], pltpu.roll(got[5], 64, 1)),
-                second(corner[0], got[1], corner[1]),
-                second(corner[2], got[3], corner[3]),
+                second([right, right_two[8:16]], own[1], [left_one, left_two[8:16]]),
+                second([right_two[16:], right_last[8:]], own[3], [left_two[16:], left[8:]]),
+                second(from_right(corner[0]), got[1], from_left(corner[1])),
+                second(from_right(corner[2]), got[3], from_left(corner[3])),
             ],
             axis=0,
         )
         return jnp.concatenate([first, other], axis=1).astype(BF)
 
     def smoothed(e, store):
-        for g in range(GROUPS):
-            part = dot(r.sxb[:, :160], assembled(e, g))
-            for k in range(5):
-                r.u_back[k, g * 112 : g * 112 + 112] = part[k * 112 : k * 112 + 112].astype(BF)
-        total = dot(r.u_back[0], r.syb[0])
-        for k in range(1, 5):
-            total = total + dot(r.u_back[k], r.syb[k])
-        for g in range(GROUPS):
-            store(g, total[g * 112 : g * 112 + 112] * r.win_mask[...])
-
-    mask = r.mask_ref[...].astype(F32).astype(BF)
+        for groups in BATCHES:
+            low, high = groups[0] * 112, groups[-1] * 112 + 112
+            for g in groups:
+                arrived(e, g)
+            for g in groups:
+                part = dot(r.sxb[:, :160], assembled(e, g))
+                for k in range(5):
+                    r.u_back[k, g * 112 : g * 112 + 112] = part[k * 112 : k * 112 + 112].astype(BF)
+            total = dot(r.u_back[0, low:high], r.syb[0])
+            for k in range(1, 5):
+                total = total + dot(r.u_back[k, low:high], r.syb[k])
+            for i, g in enumerate(groups):
+                store(g, total[i * 112 : i * 112 + 112] * r.win_mask[...])
+
+    mask = r.mask[...].astype(F32).astype(BF)
     mask_rows = dot(r.mask_x[...], mask).astype(BF)
-    send_strips(0, GROUPS, dot(mask_rows, r.mask_y[...]))
-
-    @pl.loop(0, GROUPS)
-    def _(g):
-        part = pl.ds(g * PER, PER)
-        with jax.named_scope("w_ens"):
-            pltpu.make_async_copy(r.ens_hbm.at[part], r.ens.at[part], r.ens_sem.at[g]).wait()
-        with jax.named_scope("adj0"):
+    pack_strips(0, GROUPS, dot(mask_rows, r.mask_y[...]))
+    send_strips(0, GROUPS)
+
+    for groups in BATCHES:
+        for g in groups:
+            part = pl.ds(g * PER, PER)
+            with jax.named_scope("w_ens"):
+                pltpu.make_async_copy(r.ens_hbm.at[part], r.ens.at[part], r.ens_sem.at[g]).wait()
+
+        @pl.loop(groups[0], groups[-1] + 1)
+        @jax.named_scope("adj0")
+        def _(g):
             for c in range(CHUNKS):
                 spread_rows(0, c, g)
-            coarse_send(0, g)
-
-    for name in order:
-        if name not in first:
-            loads[name].wait()
-
-    @pl.loop(0, 5)
-    @jax.named_scope("expand")
-    def _(k):
-        base = r.base[k]
-        base = jnp.concatenate([base, jnp.zeros_like(base)], axis=0)
-        to_a = dot_nt(base, r.pick_a[...]).astype(BF)
-        to_w = dot_nt(base, r.pick_w[...]).astype(BF)
-        r.syf[k] = (dot(r.pick_w[...], to_a).astype(BF) * r.same_wa[...]).astype(BF)
-        spread_f = dot(r.pick_f[...] * r.alive[...], to_w).astype(BF)
-        r.syb[k] = (spread_f * r.same_fw[...]).astype(BF)
+
+        with jax.named_scope("send0"):
+            for g in groups:
+                coarse_rows(0, g)
+            coarse_send(0, groups)
+
+    for name in order[ready:]:
+        loads[name].wait()
+    arrived(0, GROUPS)
 
     picked = dot(r.take_x[:, :160], assembled(0, GROUPS)).astype(BF)
     r.win_mask[...] = dot(picked, r.take_y[...]) * S_SCALE
@@ -550,9 +591,12 @@
             wait(r.rs_recv.at[it, CHUNKS - 1], r.agr_sem.at[it, CHUNKS - 1])
 
         with jax.named_scope("adj_send"):
-            for g in range(GROUPS):
-                spread_rows(it + 1, CHUNKS - 1, g)
-                coarse_send(it + 1, g)
+            for groups in BATCHES:
+                for g in groups:
+                    spread_rows(it + 1, CHUNKS - 1, g)
+                for g in groups:
+                    coarse_rows(it + 1, g)
+                coarse_send(it + 1, groups)
 
         r.sc_send[it, 1] = scalar_sum(it, 0, r.sc_a, len(plane))
         scalar_send(it, 1, r.sc_b, line)
@@ -579,9 +623,11 @@
         r.out_g[g] = r.grad[g, :64, :128]
 
     wait(r.h_recv.at[0], r.hs_sem.at[0])
+    wait(r.l_recv.at[0], r.ls_sem.at[0])
     wait(r.d_recv.at[0], r.ds_sem.at[0])
     for it in range(ITERS):
         wait(r.h_recv.at[it + 1, pl.ds(0, GROUPS)], r.hs_sem.at[it + 1])
+        wait(r.l_recv.at[it + 1, pl.ds(0, GROUPS)], r.ls_sem.at[it + 1])
         wait(r.d_recv.at[it + 1, pl.ds(0, GROUPS)], r.ds_sem.at[it + 1])
         wait(r.rs_recv.at[it], r.rss_sem.at[it])
         wait(r.rs_recv.at[it], r.ags_sem.at[it])
@@ -589,13 +635,28 @@
         wait(r.sc_b.at[it], r.scs_sem.at[it, 1])
 
 
-def unpack(*refs):
-    for source, out in (refs[0::2], refs[1::2]):
+def unpack(control, gradient, out_c, out_g, packed, spread, in_sem, out_sem):
+    sides = ((control, out_c), (gradient, out_g))
+    members = [pl.ds(g * PER, PER) for g in range(GROUPS)]
+    copies = [[pltpu.make_async_copy(s.at[g], packed.at[i, g], in_sem.at[i, g]) for g in range(GROUPS)] for i, (s, _) in enumerate(sides)]
+    backs = [
+        [pltpu.make_async_copy(spread.at[i, members[g]], o.at[members[g]], out_sem.at[i, g]) for g in range(GROUPS)]
+        for i, (_, o) in enumerate(sides)
+    ]
+    for i in range(2):
         for g in range(GROUPS):
+            copies[i][g].start()
+    for i in range(2):
+        for g in range(GROUPS):
+            copies[i][g].wait()
             for l in range(LEV):
-                turned = pltpu.roll(source[g], 128 - 32 * l, 1) if l else source[g]
+                turned = pltpu.roll(packed[i, g], 128 - 32 * l, 1) if l else packed[i, g]
                 for m in range(PER):
-                    out[g * PER + m, l] = turned[m * 16 : m * 16 + 16, :32]
+                    spread[i, g * PER + m, l] = turned[m * 16 : m * 16 + 16, :32]
+            backs[i][g].start()
+    for i in range(2):
+        for g in range(GROUPS):
+            backs[i][g].wait()
 
 
 def local(sizes, ensemble, huber, innovation, sea_mask):
@@ -609,6 +670,7 @@
         vmem((MEMBERS // n_mem, VARS, LEV, FINE_X, FINE_Y), BF),
         vmem((LEV, *field), F32),
         vmem((LEV, *field), F32),
+        vmem((OWN_X, OWN_Y), jnp.int32),
         *(vmem(shapes[n], BF) for n in NAMES),
         vmem((5, 256, 256), BF),
         vmem((5, 256, 256), BF),
@@ -622,19 +684,24 @@
         vmem((GROUPS * 80, 512), BF),
         vmem((LEV, GROUPS, 256, 128), BF),
         vmem((GROUPS, 256, 512), BF),
+        vmem((GROUPS * 80, 512), BF),
         vmem((times, CHUNKS, LEV, *rows), BF),
         vmem((CHUNKS, *rows), F32),
         vmem((ITERS, CHUNKS, 3, *rows), BF),
         vmem((ITERS, CHUNKS, 3, *rows), BF),
-        vmem((times, GROUPS + 1, 6, 40, 128), BF),
-        vmem((times, GROUPS + 1, 6, 40, 128), BF),
-        vmem((times, GROUPS + 1, 4, 24, 128), BF),
-        vmem((times, GROUPS + 1, 4, 24, 128), BF),
+        vmem((times, GROUPS + 1, 4, 40, 128), BF),
+        vmem((times, GROUPS + 1, 4, 40, 128), BF),
+        vmem((times, GROUPS + 1, 2, 32, 128), BF),
+        vmem((times, GROUPS + 1, 2, 32, 128), BF),
+        vmem((times, GROUPS + 1, 4, 16, 128), BF),
+        vmem((times, GROUPS + 1, 4, 16, 128), BF),
         vmem((ITERS, 2, 8, 128), F32),
         vmem((ITERS, n_mem * n_lat - 1, 8, 128), F32),
         vmem((ITERS, n_lon - 1, 8, 128), F32),
-        dma((len(NAMES) + 2,)),
+        dma((len(NAMES) + 3,)),
         dma((GROUPS,)),
+        dma((times,)),
+        dma((times, GROUPS + 1)),
         dma((times,)),
         dma((times, GROUPS + 1)),
         dma((times,)),
@@ -651,7 +718,7 @@
     control, gradient = pl.pallas_call(
         lambda *refs: kernel(sizes, *refs),
         out_shape=(packed, packed),
-        in_specs=[any_space, any_space, any_space, in_vmem, *([any_space] * len(NAMES))],
+        in_specs=[any_space] * (4 + len(NAMES)),
         out_specs=(in_vmem, in_vmem),
         scratch_shapes=scratch,
         name="assimilate",
@@ -659,7 +726,17 @@
     )(ensemble, huber, innovation, sea_mask, *(jnp.asarray(TABLES[n]) for n in NAMES))
     out = jax.ShapeDtypeStruct((MEMBERS // n_mem, LEV, OWN_X, OWN_Y), F32)
     return pl.pallas_call(
-        unpack, out_shape=(out, out), in_specs=[in_vmem] * 2, out_specs=(in_vmem, in_vmem), name="unpack"
+        unpack,
+        out_shape=(out, out),
+        in_specs=[any_space] * 2,
+        out_specs=(any_space, any_space),
+        scratch_shapes=[
+            vmem((2, *packed.shape), F32),
+            vmem((2, *out.shape), F32),
+            dma((2, GROUPS)),
+            dma((2, GROUPS)),
+        ],
+        name="unpack",
     )(control, gradient)
 
 

time: 75.1 us -> 73.4 us (0.977)
  Pallas kernels: 74.3 us -> 72.6 us
    pallas_call x1, Pallas kernels: 72 us -> 70 us  [local(): pl.pallas_call(lambda *refs: kernel(sizes, *refs), out_shape=(packed, pac...]
where the time goes in v2:
time: 73.4 us; the launch traced here: 73.2 us
  Pallas kernels  72.6 us (99%)
    pallas_call x1, Pallas kernels, local(): pl.pallas_call(lambda *refs: kernel(sizes, *refs), out_shape=(packed, pac...  70 us
    pallas_call x1, Pallas kernels, local(): pl.pallas_call(unpack, out_shape=(out, out), in_specs=[any_space] * 2, ou...  2.52 us

profile of v2, /device:TPU:1, one launch (start us, length us, event | category | flops | bytes accessed | tf_op | source)
XLA Modules:
  0.0 73.2 jit_solution(8117273121426915064)
XLA Ops:
  0.6 70.0 %assimilate.1 = (f32[5,64,128]{2,1,0:T(8,128)}, f32[5,64,128]{2,1,0:T(8,128)}) custom-call(bf16[20,4,4,64,128]{4,3,2,1,0:T(8,128)(2,1)} %refs_0_.1, f32[4,4,64,128]{3,2,1,0:T(8,128)} %refs_1_.1, f32[4,4,64,128]{3,2,1,0:T(8,128)} %refs_2_.1, s32[16,32]{1,0:T(8,128)} %refs_3_.1, bf16[3,400,128]{2,1,0:T(8,128)(2,1)} %constant.34.clone.refs_4_, ...), custom_call_target="tpu_custom_call" | custom-call | tf_op jit(solution)/shard_map/assimilate/pallas_call | solution.py:718
  70.7 2.5 %unpack.1 = (f32[20,4,16,32]{3,2,1,0:T(8,128)}, f32[20,4,16,32]{3,2,1,0:T(8,128)}) custom-call(f32[5,64,128]{2,1,0:T(8,128)} %get-tuple-element.4.control, f32[5,64,128]{2,1,0:T(8,128)} %get-tuple-element.5.gradient), custom_call_target="tpu_custom_call" | custom-call | tf_op jit(solution)/shard_map/unpack/pallas_call | solution.py:728

commit v3 on v2

--- a/solution.py
+++ b/solution.py
@@ -13,7 +13,7 @@
 MEMBERS, VARS, LEV = 80, 4, 4
 ITERS = 3
 GROUPS, PER = 5, 4
-BATCHES = ((0, 1, 2), (3, 4))
+BATCHES = ((0, 1), (2, 3, 4))
 OWN_X, OWN_Y = 16, 32
 FINE_X, FINE_Y = 64, 128
 CHUNK = 16
@@ -136,10 +136,10 @@
     same = lambda one, two: ((level(one)[:, None] == level(two)[None, :]) & (level(one)[:, None] >= 0)).astype(float)
     same_wa, same_fw = same(wl, al), same(fl, wl)
     weight_x, weight_y = hat(FINE_X), hat(FINE_Y)
-    pxf, pxt = np.zeros((256, 128)), np.zeros((80, 256))
+    pxf, pxt = np.zeros((4, 4, 16, 128)), np.zeros((80, 256))
     for j, (m, r) in enumerate(ar):
         if m >= 0:
-            pxf[m * 64 : m * 64 + 64, j] = weight_x(r)
+            pxf[:, m, :, j] = weight_x(r).reshape(4, 16)
     for j, (m, r, _) in enumerate(b_rows()):
         pxt[j, m * 64 : m * 64 + 64] = weight_x(r)
     pyf, pyt = np.zeros((256, 512)), np.zeros((512, 256))
@@ -170,18 +170,28 @@
         sxf=sxf, sxb=sxb, base=base, alive=alive, pick_w=pick_w, pick_a=pick_a, pick_f=pick_f, same_wa=same_wa,
         same_fw=same_fw, pxf=pxf, pxt=pxt, pyf=pyf, pyt=pyt, mask_x=mask_x, mask_y=mask_y, take_x=take_x, take_y=take_y,
     )
-    named.update(sxf=sxf.reshape(3, 400, 128), sxb=sxb.reshape(3, 560, 256))
+    named.update(pxf=pxf.reshape(4, 64, 128), sxf=sxf.reshape(3, 400, 128), sxb=sxb.reshape(3, 560, 256))
     return {name: np.asarray(value, np.float32).astype(BF) for name, value in named.items()}
 
 
 TABLES = tables()
 NAMES = tuple(TABLES)
 BY_LON, BY_LAT = ("sxf", "sxb"), ("base", "alive")
-SPREAD_TABLES = ("base", "alive", "pick_w", "pick_a", "pick_f", "same_wa", "same_fw")
 
 
 def dot(a, b):
     return lax.dot_general(a, b, (((1,), (0,)), ((), ())), preferred_element_type=F32)
+
+
+def summed(rows, tables, low, high):
+    middle = low + (high - low) // 32 * 16
+    halves = []
+    for start, stop in ((low, middle), (middle, high)):
+        total = dot(rows[0, start:stop], tables[0])
+        for k in range(1, 5):
+            total = total + dot(rows[k, start:stop], tables[k])
+        halves.append(total)
+    return jnp.concatenate(halves, axis=0)
 
 
 def dot_nt(a, b):
@@ -299,9 +309,8 @@
     variant_x = jnp.where(lon == 0, 0, jnp.where(lon == n_lon - 1, 2, 1))
     variant_y = jnp.where(lat == 0, 0, jnp.where(lat == n_lat - 1, 2, 1))
     loads = {}
-    early = [n for n in NAMES if n in SPREAD_TABLES]
     first = ["hub", "inn", "mask", "mask_x", "mask_y", "pxt", "pyt"]
-    order = [*early, *first, *(n for n in NAMES if n not in [*early, *first])]
+    order = [*first, *(n for n in NAMES if n not in first)]
 
     def load(i):
         name = order[i]
@@ -313,7 +322,7 @@
         loads[name] = pltpu.make_async_copy(source, getattr(r, name), r.in_sem.at[i])
         loads[name].start()
 
-    ready = len(early) + len(first)
+    ready = len(first)
     for i in range(ready):
         load(i)
     for g in range(GROUPS):
@@ -330,17 +339,6 @@
         pl.semaphore_signal(barrier, inc=1, device_id=partner, device_id_type=MESH)
 
     lane = lax.broadcasted_iota(jnp.int32, (40, 128), 1)
-    for name in early:
-        loads[name].wait()
-
-    with jax.named_scope("expand"):
-        to_a = dot_nt(r.base[...], r.pick_a[...]).astype(BF)
-        to_w = dot_nt(r.base[...], r.pick_w[...]).astype(BF)
-        for k in range(5):
-            rows = slice(k * 64, k * 64 + 64)
-            r.syf[k] = dot(r.pick_w[:, :64], to_a[rows]).astype(BF) * r.same_wa[...]
-            r.syb[k] = dot(r.pick_f[:, :64] * r.alive[:, :64], to_w[rows]).astype(BF) * r.same_fw[...]
-
     for name in first:
         loads[name].wait()
 
@@ -449,9 +447,7 @@
                 part = dot(r.sxb[:, :160], assembled(e, g))
                 for k in range(5):
                     r.u_back[k, g * 112 : g * 112 + 112] = part[k * 112 : k * 112 + 112].astype(BF)
-            total = dot(r.u_back[0, low:high], r.syb[0])
-            for k in range(1, 5):
-                total = total + dot(r.u_back[k, low:high], r.syb[k])
+            total = summed(r.u_back, r.syb, low, high)
             for i, g in enumerate(groups):
                 store(g, total[i * 112 : i * 112 + 112] * r.win_mask[...])
 
@@ -479,6 +475,15 @@
 
     for name in order[ready:]:
         loads[name].wait()
+
+    with jax.named_scope("expand"):
+        to_a = dot_nt(r.base[...], r.pick_a[...]).astype(BF)
+        to_w = dot_nt(r.base[...], r.pick_w[...]).astype(BF)
+        for k in range(5):
+            rows = slice(k * 64, k * 64 + 64)
+            r.syf[k] = dot(r.pick_w[:, :64], to_a[rows]).astype(BF) * r.same_wa[...]
+            r.syb[k] = dot(r.pick_f[:, :64] * r.alive[:, :64], to_w[rows]).astype(BF) * r.same_fw[...]
+
     arrived(0, GROUPS)
 
     picked = dot(r.take_x[:, :160], assembled(0, GROUPS)).astype(BF)
@@ -517,27 +522,24 @@
                 part = dot(r.sxf[:, :112], r.grad[g].astype(BF))
                 for k in range(5):
                     r.u_fwd[k, g * 80 : g * 80 + 80] = part[k * 80 : k * 80 + 80].astype(BF)
-            total = dot(r.u_fwd[0], r.syf[0])
-            for k in range(1, 5):
-                total = total + dot(r.u_fwd[k], r.syf[k])
+            total = summed(r.u_fwd, r.syf, 0, GROUPS * 80)
             r.coarse[...] = (total * S_SCALE).astype(BF)
             r.fine[...] = dot(r.coarse[...], r.pyf[...]).astype(BF)
-            for g in range(GROUPS):
-                part = dot(r.pxf[:, :80], r.fine[g * 80 : g * 80 + 80]).astype(BF)
-                for l in range(LEV):
-                    r.wbuf[l, g] = part[:, l * 128 : l * 128 + 128]
 
         @pl.loop(0, CHUNKS)
         @jax.named_scope("inc")
         def _(c):
-            start = pl.multiple_of(c * CHUNK, CHUNK)
-            rows = pl.ds(start, CHUNK)
+            rows = pl.ds(pl.multiple_of(c * CHUNK, CHUNK), CHUNK)
+            for g in range(GROUPS):
+                part = dot(r.pxf[c, :, :80], r.fine[g * 80 : g * 80 + 80]).astype(BF)
+                for l in range(LEV):
+                    r.wbuf[c, l, g] = part[:, l * 128 : l * 128 + 128]
             for step, away in enumerate((2, 1, 3, 0)):
                 level = lax.rem(mem + away, n_mem)
                 sums = [jnp.zeros((CHUNK, 128), F32) for _ in range(VARS)]
                 for m in range(GROUPS * PER):
-                    place = pl.ds(pl.multiple_of((m % PER) * 64 + start, CHUNK), CHUNK)
-                    weight = r.wbuf[level, m // PER, place].astype(F32)
+                    place = slice(m % PER * CHUNK, m % PER * CHUNK + CHUNK)
+                    weight = r.wbuf[c, level, m // PER, place].astype(F32)
                     for v in range(VARS):
                         sums[v] = sums[v] + r.ens[m, v, level, rows].astype(F32) * weight
                 for v in range(VARS):
@@ -635,28 +637,19 @@
         wait(r.sc_b.at[it], r.scs_sem.at[it, 1])
 
 
-def unpack(control, gradient, out_c, out_g, packed, spread, in_sem, out_sem):
-    sides = ((control, out_c), (gradient, out_g))
-    members = [pl.ds(g * PER, PER) for g in range(GROUPS)]
-    copies = [[pltpu.make_async_copy(s.at[g], packed.at[i, g], in_sem.at[i, g]) for g in range(GROUPS)] for i, (s, _) in enumerate(sides)]
-    backs = [
-        [pltpu.make_async_copy(spread.at[i, members[g]], o.at[members[g]], out_sem.at[i, g]) for g in range(GROUPS)]
-        for i, (_, o) in enumerate(sides)
-    ]
-    for i in range(2):
+def unpack(control, gradient, out_c, out_g, spread, out_sem):
+    backs = []
+    for i, (packed, out) in enumerate(((control, out_c), (gradient, out_g))):
         for g in range(GROUPS):
-            copies[i][g].start()
-    for i in range(2):
-        for g in range(GROUPS):
-            copies[i][g].wait()
             for l in range(LEV):
-                turned = pltpu.roll(packed[i, g], 128 - 32 * l, 1) if l else packed[i, g]
+                turned = pltpu.roll(packed[g], 128 - 32 * l, 1) if l else packed[g]
                 for m in range(PER):
                     spread[i, g * PER + m, l] = turned[m * 16 : m * 16 + 16, :32]
-            backs[i][g].start()
-    for i in range(2):
-        for g in range(GROUPS):
-            backs[i][g].wait()
+            members = pl.ds(g * PER, PER)
+            backs.append(pltpu.make_async_copy(spread.at[i, members], out.at[members], out_sem.at[i, g]))
+            backs[-1].start()
+    for back in backs:
+        back.wait()
 
 
 def local(sizes, ensemble, huber, innovation, sea_mask):
@@ -682,7 +675,7 @@
         vmem((5, GROUPS * 112, 256), BF),
         vmem((GROUPS * 80, 256), BF),
         vmem((GROUPS * 80, 512), BF),
-        vmem((LEV, GROUPS, 256, 128), BF),
+        vmem((CHUNKS, LEV, GROUPS, 64, 128), BF),
         vmem((GROUPS, 256, 512), BF),
         vmem((GROUPS * 80, 512), BF),
         vmem((times, CHUNKS, LEV, *rows), BF),
@@ -717,8 +710,8 @@
     any_space, in_vmem = pl.BlockSpec(memory_space=pl.ANY), pl.BlockSpec(memory_space=pltpu.VMEM)
     control, gradient = pl.pallas_call(
         lambda *refs: kernel(sizes, *refs),
-        out_shape=(packed, packed),
-        in_specs=[any_space] * (4 + len(NAMES)),
+        out_shape=(vmem(packed.shape, F32),) * 2,
+        in_specs=[pl.BlockSpec(memory_space=pltpu.HBM)] * (4 + len(NAMES)),
         out_specs=(in_vmem, in_vmem),
         scratch_shapes=scratch,
         name="assimilate",
@@ -728,15 +721,14 @@
     return pl.pallas_call(
         unpack,
         out_shape=(out, out),
-        in_specs=[any_space] * 2,
+        in_specs=[in_vmem] * 2,
         out_specs=(any_space, any_space),
         scratch_shapes=[
-            vmem((2, *packed.shape), F32),
             vmem((2, *out.shape), F32),
-            dma((2, GROUPS)),
             dma((2, GROUPS)),
         ],
         name="unpack",
+        compiler_params=pltpu.CompilerParams(vmem_limit_bytes=8 * 2**20),
     )(control, gradient)
 
 

time: 73.4 us -> 68.3 us (0.931)
  Pallas kernels: 72.6 us -> 67.6 us
    pallas_call x2, Pallas kernels: 72.6 us -> 67.6 us  [the longest x1 66.3 us: local(): pl.pallas_call(lambda *refs: kernel(sizes, *refs), out_shape=(vmem(packed...]
where the time goes in v3:
time: 68.3 us; the launch traced here: 68.2 us
  Pallas kernels  67.6 us (99%)
    pallas_call x1, Pallas kernels, local(): pl.pallas_call(lambda *refs: kernel(sizes, *refs), out_shape=(vmem(packed...  66.3 us

profile of v3, /device:TPU:1, one launch (start us, length us, event | category | flops | bytes accessed | tf_op | source)
XLA Modules:
  0.0 68.2 jit_solution(1448841050463648945)
XLA Ops:
  0.6 66.3 %assimilate.1 = (f32[5,64,128]{2,1,0:T(8,128)S(1)}, f32[5,64,128]{2,1,0:T(8,128)S(1)}) custom-call(bf16[20,4,4,64,128]{4,3,2,1,0:T(8,128)(2,1)} %refs_0_.1, f32[4,4,64,128]{3,2,1,0:T(8,128)} %refs_1_.1, f32[4,4,64,128]{3,2,1,0:T(8,128)} %refs_2_.1, s32[16,32]{1,0:T(8,128)} %refs_3_.1, bf16[3,400,128]{2,1,0:T(8,128)(2,1)} %constant.34.clone.refs_4_, ...), custom_call_target="tpu_custom_call" | custom-call | tf_op jit(solution)/shard_map/assimilate/pallas_call | solution.py:711
  67.0 1.2 %unpack.1 = (f32[20,4,16,32]{3,2,1,0:T(8,128)}, f32[20,4,16,32]{3,2,1,0:T(8,128)}) custom-call(f32[5,64,128]{2,1,0:T(8,128)S(1)} %get-tuple-element.4.control, f32[5,64,128]{2,1,0:T(8,128)S(1)} %get-tuple-element.5.gradient), custom_call_target="tpu_custom_call" | custom-call | tf_op jit(solution)/shard_map/unpack/pallas_call | solution.py:721
